TPU v7x, 256 devices: a whole 4x4x8 slice. The times are simulated.
256 devices in a mesh: section: 8 (over y_hi, x), expert: 32 (over y_lo, z, core).
Axes of the slice: x: 4, y: 4 (y_hi: 2, y_lo: 2; y = y_hi * 2 + y_lo), z: 8, core: 2. Of those that a mesh axis runs over, the one named last changes fastest.
Arguments:
- initial_batch: bfloat16 [8, 2048, 4096], P('section', 'expert'), may hold values from -6 to 6
- arriving_batches: bfloat16 [1, 2048, 4096], P(None, 'expert'), may hold values from -6 to 6
- rescaling_gains: float32 [8, 4096], P('section'), may hold values from 0.5 to 2
- gating_projection: bfloat16 [8, 4096, 14336], P('section', None, 'expert'), may hold values from -0.09375 to 0.09375
- expanding_projection: bfloat16 [8, 4096, 14336], P('section', None, 'expert'), may hold values from -0.09375 to 0.09375
- contracting_projection: bfloat16 [8, 14336, 4096], P('section', 'expert'), may hold values from -0.0625 to 0.0625
- routed_specialist_pairs: int32 [8, 2, 2048, 2], P('section', None, 'expert'), may hold values from 0 to 7, all different within a row; in each aligned block of 64 rows (0 to 63, 64 to 127, ..., all dimensions but the last counted through in order) at most 20 rows name the same one
- primary_routing_share: float32 [8, 2, 2048], P('section', None, 'expert'), may hold values from 0.1 to 0.9
Outputs:
- states: bfloat16 [8, 2, 2048, 4096], P('section', None, 'expert')
Inputs may be any that keep to these rules, and one draw needn't show every extreme that they name: `routed_specialist_pairs`: A token's two ids differ. In each aligned block of 64 rows (one device's tokens at one layer and microbatch) no expert is named by more than 20 tokens.
All inputs are finite; a program needn't handle non-finite values.
Results may differ from a plain program's by a relative error of at most 0.009.
Values may be sent and summed in bfloat16 or wider, within the bound.
No kernel may reach another device: no remote copies, remote signals or barrier semaphores. Data moves between devices by JAX's collectives and lax.ppermute only.
A program may use at most 128 MiB of HBM per device.

v0:
```python
import jax
import jax.numpy as jnp
from jax import lax
from jax.sharding import PartitionSpec as P

EXP_WIN = 2
TICKS = 2
CAP = 20


def passed_along(x, axis, by):
    length = lax.axis_size(axis)
    pairs = [(i, i + by) for i in range(length) if 0 <= i + by < length]
    return lax.ppermute(x, axis, pairs)


def routing_tables(token_ids, share, capacity):
    count = token_ids.shape[0]
    flat_ids = token_ids.reshape(-1)
    member = (flat_ids[:, None] == jnp.arange(EXP_WIN)[None, :]).astype(jnp.int32)
    position = jnp.cumsum(member, axis=0) - 1
    slot_index = jnp.sum(position * member, axis=1)
    target = flat_ids * capacity + slot_index
    placed = (target[:, None] == jnp.arange(EXP_WIN * capacity)[None, :]).astype(jnp.float32)
    owners = jnp.arange(2 * count) // 2
    owner_hot = (owners[:, None] == jnp.arange(count)[None, :]).astype(jnp.float32)
    dispatch_table = jnp.dot(placed.T, owner_hot, preferred_element_type=jnp.float32).astype(
        jnp.bfloat16
    )
    shares = jnp.stack([share, 1.0 - share], axis=-1).reshape(-1)
    combine_table = jnp.dot((owner_hot * shares[:, None]).T, placed)
    return (dispatch_table, combine_table)


def shards(
    initial_batch,
    arriving_batches,
    rescaling_gains,
    gating_projection,
    expanding_projection,
    contracting_projection,
    routed_specialist_pairs,
    primary_routing_share,
):
    devices = lax.axis_size("expert")
    group = devices // EXP_WIN
    capacity = CAP
    section_pos = lax.axis_index("section")
    gain = rescaling_gains[0]
    gate_cols = gating_projection[0]
    up_cols = expanding_projection[0]
    down_rows = contracting_projection[0]
    feedforward_breadth = initial_batch.shape[2]
    current_activation = initial_batch[0]
    results = []
    for tick in range(TICKS):
        widened = current_activation.astype(jnp.float32)
        scale = lax.rsqrt(jnp.mean(widened * widened, axis=-1, keepdims=True) + 1e-06)
        normed = (widened * scale * gain).astype(jnp.bfloat16)
        dispatch_table, combine_table = routing_tables(
            routed_specialist_pairs[0, tick], primary_routing_share[0, tick], capacity
        )
        send_rows = jnp.dot(dispatch_table, normed, preferred_element_type=jnp.float32).astype(
            jnp.bfloat16
        )
        copies = jnp.broadcast_to(
            send_rows.reshape(EXP_WIN, 1, capacity, feedforward_breadth),
            (EXP_WIN, group, capacity, feedforward_breadth),
        )
        copies = copies.reshape(EXP_WIN * group, capacity, feedforward_breadth)
        moe_received = lax.all_to_all(copies, "expert", split_axis=0, concat_axis=0, tiled=True)
        sources, slots, width = moe_received.shape
        flat_rows = moe_received.reshape(sources * slots, width)
        gate_pre = jnp.dot(flat_rows, gate_cols, preferred_element_type=jnp.float32)
        up_pre = jnp.dot(flat_rows, up_cols, preferred_element_type=jnp.float32)
        hidden = (jax.nn.silu(gate_pre) * up_pre).astype(jnp.bfloat16)
        partial_value = jnp.dot(hidden, down_rows, preferred_element_type=jnp.float32).astype(
            jnp.bfloat16
        )
        returned = lax.all_to_all(
            partial_value.reshape(sources, slots, width),
            "expert",
            split_axis=0,
            concat_axis=0,
            tiled=True,
        )
        summed = jnp.sum(
            returned.reshape(EXP_WIN, group, capacity, feedforward_breadth).astype(jnp.float32),
            axis=1,
        )
        mixture = jnp.dot(combine_table, summed.reshape(EXP_WIN * capacity, feedforward_breadth))
        mixture = mixture.astype(jnp.bfloat16)
        layer_out = (widened + mixture.astype(jnp.float32)).astype(jnp.bfloat16)
        layer_out, mixture = (layer_out, mixture)
        results.append(layer_out)
        if tick + 1 < TICKS:
            passed = passed_along(layer_out, "section", 1)
            current_activation = jnp.where(section_pos == 0, arriving_batches[tick], passed)
    return jnp.stack(results)[None]


def solution(mesh):
    return jax.shard_map(
        shards,
        mesh=mesh,
        in_specs=(
            P("section", "expert", None),
            P(None, "expert", None),
            P("section", None),
            P("section", None, "expert"),
            P("section", None, "expert"),
            P("section", "expert", None),
            P("section", None, "expert", None),
            P("section", None, "expert"),
        ),
        out_specs=P("section", None, "expert", None),
        check_vma=False,
    )
```

profile of v0, /device:TPU:16, one launch (start us, length us, event | category | flops | bytes accessed | tf_op | source)
XLA Modules:
  0.0 699.7 jit_solution(261869998334414080)
XLA Ops:
  0.0 1.2 fusion.36
  1.3 0.7 fusion.86
  2.7 1.5 convolution_convert_fusion.5
  4.3 0.8 broadcast_in_dim.11
  5.1 150.3 %all_to_all.20 = bf16[32,20,4096]{2,1,0:T(8,128)(2,1)} all-to-all(bf16[32,20,4096]{2,1,0:T(8,128)(2,1)S(1)} %bitcast.70), channel_id=1, replica_groups=mesh['section'=8,'expert'=32] {'expert'}, dimensions={0} | all-to-all | bytes 10485760 | tf_op jit(solution)/shard_map/all_to_all | solution.py:71
  155.4 7.8 %reshape.106 = bf16[640,4096]{1,0:T(8,128)(2,1)} reshape(bf16[32,20,4096]{2,1,0:T(8,128)(2,1)} %all_to_all.20) | data formatting | bytes 10485760 | tf_op jit(solution)/shard_map/reshape | solution.py:73
  163.2 6.6 fusion.15
  169.9 14.8 %convolution_convert_fusion.1 = bf16[640,4096]{1,0:T(8,128)(2,1)} fusion(bf16[1,448,4096]{2,1,0:T(8,128)(2,1)} %param.13, bf16[640,4096]{1,0:T(8,128)(2,1)} %reshape.106, bf16[1,4096,448]{1,2,0:T(8,128)(2,1)} %param.12, f32[640,448]{0,1:T(8,128)S(1)} %fusion.15), kind=kOutput, calls=%fused_computation.3 | convolution fusion | flops 4701962240 | bytes 18972672 | tf_op jit(solution)/shard_map/dot_general | solution.py:77
  184.7 7.7 %reshape.107 = bf16[32,20,4096]{2,1,0:T(8,128)(2,1)} reshape(bf16[640,4096]{1,0:T(8,128)(2,1)} %convolution_convert_fusion.1) | data formatting | bytes 10485760 | tf_op jit(solution)/shard_map/reshape | solution.py:81
  192.4 5.2 all-to-all-start.1
  198.2 140.1 %all-to-all-done.1 = bf16[32,20,4096]{2,1,0:T(8,128)(2,1)} async-done(((bf16[32,20,4096]{2,1,0:T(8,128)(2,1)}), bf16[32,20,4096]{2,1,0:T(8,128)(2,1)}, u32[]{:S(2)}, u32[]{:S(2)}) %all-to-all-start.1) | async-done | bytes 5242912 | tf_op jit(solution)/shard_map/all_to_all | solution.py:80
  338.3 3.9 convert_reduce_fusion.1
  342.9 3.4 collective-permute-start
  346.7 14.1 %collective-permute-done = bf16[64,4096]{1,0:T(8,128)(2,1)S(1)} collective-permute-done((bf16[64,4096]{1,0:T(8,128)(2,1)S(1)}, bf16[64,4096]{1,0:T(8,128)(2,1)S(1)}, u32[]{:S(2)}, u32[]{:S(2)}) %collective-permute-start) | collective-permute-done | bytes 524320 | tf_op jit(solution)/shard_map/ppermute | solution.py:14
  361.7 0.8 broadcast_in_dim.13
  362.5 148.9 %all_to_all.21 = bf16[32,20,4096]{2,1,0:T(8,128)(2,1)} all-to-all(bf16[32,20,4096]{2,1,0:T(8,128)(2,1)S(1)} %bitcast.71), channel_id=1, replica_groups=mesh['section'=8,'expert'=32] {'expert'}, dimensions={0} | all-to-all | bytes 10485760 | tf_op jit(solution)/shard_map/all_to_all | solution.py:71
  511.4 7.8 %reshape.110 = bf16[640,4096]{1,0:T(8,128)(2,1)} reshape(bf16[32,20,4096]{2,1,0:T(8,128)(2,1)} %all_to_all.21) | data formatting | bytes 10485760 | tf_op jit(solution)/shard_map/reshape | solution.py:73
  519.2 6.6 fusion.13
  525.9 14.8 %convolution_convert_fusion = bf16[640,4096]{1,0:T(8,128)(2,1)} fusion(bf16[1,448,4096]{2,1,0:T(8,128)(2,1)} %param.13, bf16[640,4096]{1,0:T(8,128)(2,1)} %reshape.110, bf16[1,4096,448]{1,2,0:T(8,128)(2,1)} %param.12, f32[640,448]{0,1:T(8,128)S(1)} %fusion.13), kind=kOutput, calls=%fused_computation.2 | convolution fusion | flops 4701962240 | bytes 18972672 | tf_op jit(solution)/shard_map/dot_general | solution.py:77
  540.7 7.7 %reshape.111 = bf16[32,20,4096]{2,1,0:T(8,128)(2,1)} reshape(bf16[640,4096]{1,0:T(8,128)(2,1)} %convolution_convert_fusion) | data formatting | bytes 10485760 | tf_op jit(solution)/shard_map/reshape | solution.py:81
  548.4 4.9 all-to-all-start.3
  553.5 140.6 %all-to-all-done.3 = bf16[32,20,4096]{2,1,0:T(8,128)(2,1)} async-done(((bf16[32,20,4096]{2,1,0:T(8,128)(2,1)}), bf16[32,20,4096]{2,1,0:T(8,128)(2,1)}, u32[]{:S(2)}, u32[]{:S(2)}) %all-to-all-start.3) | async-done | bytes 5242912 | tf_op jit(solution)/shard_map/all_to_all | solution.py:80
  694.1 3.9 convert_reduce_fusion
  698.7 1.1 maximum_bitcast_fusion
  (37 shorter events, 4.1 us)
Async XLA Ops:
  192.4 5.2 copy-start.2
  192.4 145.9 %all-to-all-start.1 = ((bf16[32,20,4096]{2,1,0:T(8,128)(2,1)}), bf16[32,20,4096]{2,1,0:T(8,128)(2,1)}, u32[]{:S(2)}, u32[]{:S(2)}) async-start(bf16[32,20,4096]{2,1,0:T(8,128)(2,1)} %reshape.107), calls=%async_computation.1 | async-start | bytes 12582912 | tf_op jit(solution)/shard_map/all_to_all | solution.py:80
  198.2 144.1 %copy-start = (bf16[1,64,4096]{2,1,0:T(8,128)(2,1)S(1)}, bf16[1,64,4096]{2,1,0:T(8,128)(2,1)}, u32[]{:S(2)}) copy-start(bf16[1,64,4096]{2,1,0:T(8,128)(2,1)} %param.8) | copy-start | bytes 1572868
  198.2 162.6 %copy-start.1 = (bf16[1,64,4096]{2,1,0:T(8,128)(2,1)S(1)}, bf16[1,64,4096]{2,1,0:T(8,128)(2,1)}, u32[]{:S(2)}) copy-start(bf16[1,64,4096]{2,1,0:T(8,128)(2,1)} %param.9) | copy-start | bytes 1572868
  198.2 162.9 %copy-start.3 = (f32[1,4096]{1,0:T(1,128)S(1)}, f32[1,4096]{1,0:T(1,128)}, u32[]{:S(2)}) copy-start(f32[1,4096]{1,0:T(1,128)} %param.10) | copy-start | bytes 49156
  342.9 17.9 %collective-permute-start = (bf16[64,4096]{1,0:T(8,128)(2,1)S(1)}, bf16[64,4096]{1,0:T(8,128)(2,1)S(1)}, u32[]{:S(2)}, u32[]{:S(2)}) collective-permute-start(bf16[64,4096]{1,0:T(8,128)(2,1)S(1)} %fusion.4), channel_id=1, source_target_pairs={{0,32},{32,64},{64,96},{96,128},{128,160},{160,192},{192,224},{1,3... | collective-permute-start | bytes 1572872 | tf_op jit(solution)/shard_map/ppermute | solution.py:14
  548.4 145.8 %all-to-all-start.3 = ((bf16[32,20,4096]{2,1,0:T(8,128)(2,1)}), bf16[32,20,4096]{2,1,0:T(8,128)(2,1)}, u32[]{:S(2)}, u32[]{:S(2)}) async-start(bf16[32,20,4096]{2,1,0:T(8,128)(2,1)} %reshape.111), calls=%async_computation.3 | async-start | bytes 12582912 | tf_op jit(solution)/shard_map/all_to_all | solution.py:80
where the time goes:
time: 701 us; the launch traced here: 700 us
  blocking collectives  299 us (43%)
  waiting for transfers between devices  295 us (42%)
  matrix products  46.1 us (7%)
  local copies, waits for them, and re-layouts  34.6 us (5%)
  starting transfers between devices  13.5 us (2%)
  other arithmetic  11.3 us (2%)
    all_to_all x2, blocking collectives, shards(): lax.all_to_all(copies, 'expert', split_axis=0, concat_axis=0, tiled=True)  299 us
    all_to_all x2, waiting for transfers between devices, shards(): lax.all_to_all(partial_value.reshape(sources, slots, width), 'expert', sp...  281 us
    dot_general x2, matrix products, shards(): jnp.dot(hidden, down_rows, preferred_element_type=jnp.float32)  29.6 us
    reshape x2, local copies, waits for them, and re-layouts, shards(): flat_rows = moe_received.reshape(sources * slots, width)  15.7 us
    reshape x2, local copies, waits for them, and re-layouts, shards(): partial_value.reshape(sources, slots, width)  15.4 us
    ppermute x1, waiting for transfers between devices, passed_along(): return lax.ppermute(x, axis, pairs)  14.1 us
  transfers between devices with their start and end apart: 3, of which 3 were waited for; matrix products, arithmetic and copies ran while one was open for 0% of the time, Pallas kernels for 0%

commit v1 on v0

v1 whole, which is shorter than its diff:
```python
import jax
import jax.numpy as jnp
from jax import lax
from jax.sharding import Mesh, PartitionSpec as P

EXP_WIN = 2
TICKS = 2
CAP = 20


def routing_tables(token_ids, share, experts):
    count = token_ids.shape[0]
    flat_ids = token_ids.reshape(-1)
    member = (flat_ids[:, None] == experts[None, :]).astype(jnp.int32)
    position = jnp.cumsum(member, axis=0) - 1
    slot_index = jnp.sum(position * member, axis=1)
    which = jnp.sum(member * jnp.arange(EXP_WIN)[None, :], axis=1)
    valid = jnp.sum(member, axis=1) > 0
    target = jnp.where(valid, which * CAP + slot_index, -1)
    placed = (target[:, None] == jnp.arange(EXP_WIN * CAP)[None, :]).astype(jnp.float32)
    placed = placed.reshape(count, 2, EXP_WIN * CAP)
    dispatch_table = jnp.sum(placed, axis=1).T.astype(jnp.bfloat16)
    combine_table = placed[:, 0] * share[:, None] + placed[:, 1] * (1.0 - share)[:, None]
    return dispatch_table, combine_table


def shards(initial, arriving, gains, gate_w, up_w, down_w, pairs, shares):
    section_pos = lax.axis_index("section")
    y_pos = lax.axis_index("y")
    gain = gains[0]
    gate_cols = gate_w[0]
    up_cols = up_w[0]
    down_rows = down_w[0]
    current = initial[0]
    experts = jnp.stack([y_pos, 1 - y_pos]).astype(jnp.int32)
    swap = [(0, 1), (1, 0)]
    n_sec = lax.axis_size("section")
    fwd = [(i, i + 1) for i in range(n_sec - 1)]
    results = []
    for tick in range(TICKS):
        widened = current.astype(jnp.float32)
        scale = lax.rsqrt(jnp.mean(widened * widened, axis=-1, keepdims=True) + 1e-06)
        normed = (widened * scale * gain).astype(jnp.bfloat16)
        disp, comb = routing_tables(pairs[0, tick], shares[0, tick], experts)
        send_rows = jnp.dot(disp, normed, preferred_element_type=jnp.float32).astype(jnp.bfloat16)
        own, other = send_rows[:CAP], send_rows[CAP:]
        got = lax.ppermute(other, "y", swap)
        block = jnp.concatenate([own, got], axis=0)
        rows = lax.all_gather(block, ("z", "core"), axis=0, tiled=True)
        gate_pre = jnp.dot(rows, gate_cols, preferred_element_type=jnp.float32)
        up_pre = jnp.dot(rows, up_cols, preferred_element_type=jnp.float32)
        hidden = (jax.nn.silu(gate_pre) * up_pre).astype(jnp.bfloat16)
        partial = jnp.dot(hidden, down_rows, preferred_element_type=jnp.float32).astype(jnp.bfloat16)
        summed = lax.psum_scatter(partial, ("z", "core"), scatter_dimension=0, tiled=True)
        back = lax.ppermute(summed[CAP:], "y", swap)
        both = jnp.concatenate([summed[:CAP], back], axis=0)
        mixture = jnp.dot(comb, both.astype(jnp.float32), precision=lax.Precision.HIGHEST)
        mixture = mixture.astype(jnp.bfloat16)
        layer_out = (widened + mixture.astype(jnp.float32)).astype(jnp.bfloat16)
        results.append(layer_out)
        if tick + 1 < TICKS:
            passed = lax.ppermute(layer_out, "section", fwd)
            current = jnp.where(section_pos == 0, arriving[tick], passed)
    return jnp.stack(results)[None]


def solution(mesh):
    devices = mesh.devices
    n_sec = devices.shape[0]
    m = Mesh(devices.reshape(n_sec, 2, devices.shape[1] // 4, 2), ("section", "y", "z", "core"))
    ex = ("y", "z", "core")
    return jax.shard_map(
        shards,
        mesh=m,
        in_specs=(
            P("section", ex, None),
            P(None, ex, None),
            P("section", None),
            P("section", None, ex),
            P("section", None, ex),
            P("section", ex, None),
            P("section", None, ex, None),
            P("section", None, ex),
        ),
        out_specs=P("section", None, ex, None),
        check_vma=False,
    )
```

time: 701 us -> 324 us (0.46)
  blocking collectives: 299 us -> 0 us
  waiting for transfers between devices: 295 us -> 246 us
  local copies, waits for them, and re-layouts: 34.6 us -> 4.41 us
  between operations: 0.26 us -> 13.3 us
    all_to_all x2 -> x0, blocking collectives: 299 us -> none  [shards(): lax.all_to_all(copies, 'expert', split_axis=0, concat_axis=0, tiled=True)]
    all_to_all x2 -> x0, waiting for transfers between devices: 281 us -> none  [shards(): lax.all_to_all(partial_value.reshape(sources, slots, width), 'expert', sp...]
    reduce_scatter x0 -> x2, waiting for transfers between devices: none -> 127 us  [shards(): lax.psum_scatter(partial, ('z', 'core'), scatter_dimension=0, tiled=True)]
    all_gather x0 -> x2, waiting for transfers between devices: none -> 89 us  [shards(): rows = lax.all_gather(block, ('z', 'core'), axis=0, tiled=True)]
    reshape x6 -> x0, local copies, waits for them, and re-layouts: 31.2 us -> none  [the longest x2 15.7 us: shards(): flat_rows = moe_received.reshape(sources * slots, width)]
    ppermute x1 -> x5, waiting for transfers between devices: 14.1 us -> 30.1 us  [the longest x1 11.2 us: shards(): passed = lax.ppermute(layer_out, 'section', fwd)]
    all_to_all x2 -> x0, starting transfers between devices: 10.1 us -> none  [shards(): lax.all_to_all(partial_value.reshape(sources, slots, width), 'expert', sp...]
    reduce_sum x4 -> x3, other arithmetic: 8.14 us -> 0.3 us  [the longest x1 0.25 us: routing_tables(): which = jnp.sum(member * jnp.arange(EXP_WIN)[None, :], axis=1)]
  transfers between devices with their start and end apart: 3 -> 9, of which waited for: 3 -> 9; matrix products, arithmetic and copies ran while one was open for 0% -> 0% of each run, Pallas kernels for 0% -> 0%
where the time goes in v1:
time: 324 us
  waiting for transfers between devices  246 us (76%)
  matrix products  45.8 us (14%)
  between operations  13.3 us (4%)
  starting transfers between devices  8.82 us (3%)
  other arithmetic  5.03 us (2%)
  local copies, waits for them, and re-layouts  4.41 us (1%)
    reduce_scatter x2, waiting for transfers between devices, shards(): lax.psum_scatter(partial, ('z', 'core'), scatter_dimension=0, tiled=True)  127 us
    all_gather x2, waiting for transfers between devices, shards(): rows = lax.all_gather(block, ('z', 'core'), axis=0, tiled=True)  89 us
    dot_general x2, matrix products, shards(): jnp.dot(hidden, down_rows, preferred_element_type=jnp.float32)  29.5 us
    dot_general x2, matrix products, shards(): up_pre = jnp.dot(rows, up_cols, preferred_element_type=jnp.float32)  13.3 us
    ppermute x1, waiting for transfers between devices, shards(): passed = lax.ppermute(layer_out, 'section', fwd)  11.2 us
    ppermute x2, waiting for transfers between devices, shards(): got = lax.ppermute(other, 'y', swap)  9.74 us
    ppermute x2, waiting for transfers between devices, shards(): back = lax.ppermute(summed[CAP:], 'y', swap)  9.09 us
  transfers between devices with their start and end apart: 9, of which 9 were waited for; matrix products, arithmetic and copies ran while one was open for 0% of the time, Pallas kernels for 0%

profile of v1, /device:TPU:16, one launch (start us, length us, event | category | flops | bytes accessed | tf_op | source)
XLA Modules:
  0.0 323.8 jit_solution(1592737780683528862)
XLA Ops:
  8.8 1.2 fusion.20
  10.0 1.4 convolution_convert_fusion.5
  11.5 1.4 collective-permute-start
  12.8 5.4 %collective-permute-done = bf16[20,4096]{1,0:T(8,128)(2,1)S(1)} collective-permute-done((bf16[20,4096]{1,0:T(8,128)(2,1)S(1)}, bf16[20,4096]{1,0:T(8,128)(2,1)S(1)}, u32[]{:S(2)}, u32[]{:S(2)}) %collective-permute-start) | collective-permute-done | bytes 163872 | tf_op jit(solution)/shard_map/ppermute | solution.py:47
  18.2 0.8 pad_maximum_fusion
  19.1 46.1 %all-gather.3.cloned.1.call-done = bf16[640,4096]{1,0:T(8,128)(2,1)} async-done(((bf16[40,4096]{1,0:T(8,128)(2,1)}), bf16[640,4096]{1,0:T(8,128)(2,1)}) %all-gather.3.cloned.1.call-update) | async-done | bytes 5242896 | tf_op jit(solution)/shard_map/all_gather | solution.py:49
  65.1 6.6 %fusion.11 = f32[640,448]{0,1:T(8,128)S(1)} fusion(bf16[640,4096]{1,0:T(8,128)(2,1)} %all-gather.3.cloned.1.call-done, bf16[1,4096,448]{1,2,0:T(8,128)(2,1)} %param.12), kind=kOutput, calls=%fused_computation.17 | convolution fusion | flops 2348810240 | bytes 10059776 | tf_op jit(solution)/shard_map/dot_general | solution.py:51
  71.8 14.8 %convolution_convert_fusion.1 = bf16[640,4096]{1,0:T(8,128)(2,1)} fusion(bf16[1,448,4096]{2,1,0:T(8,128)(2,1)} %param.13, f32[640,448]{0,1:T(8,128)S(1)} %fusion.11, bf16[640,4096]{1,0:T(8,128)(2,1)} %all-gather.3.cloned.1.call-done, bf16[1,4096,448]{1,2,0:T(8,128)(2,1)} %param.11), kind=kOutput, calls=%fused_computation.1 | convolution fusion | flops 4701962240 | bytes 18972672 | tf_op jit(solution)/shard_map/dot_general | solution.py:53
  87.2 63.3 %reduce-scatter.3.cloned.1.call-done = bf16[40,4096]{1,0:T(8,128)(2,1)} async-done(((bf16[640,4096]{1,0:T(8,128)(2,1)}), bf16[40,4096]{1,0:T(8,128)(2,1)}) %reduce-scatter.3.cloned.1.call-update) | async-done | bytes 327696 | tf_op jit(solution)/shard_map/reduce_scatter | solution.py:54
  150.5 1.1 fusion.78
  151.6 1.5 collective-permute-start.1
  153.1 4.4 %collective-permute-done.1 = bf16[20,4096]{1,0:T(8,128)(2,1)S(1)} collective-permute-done((bf16[20,4096]{1,0:T(8,128)(2,1)S(1)}, bf16[20,4096]{1,0:T(8,128)(2,1)S(1)}, u32[]{:S(2)}, u32[]{:S(2)}) %collective-permute-start.1) | collective-permute-done | bytes 163872 | tf_op jit(solution)/shard_map/ppermute | solution.py:55
  158.2 3.4 %collective-permute-start.2 = (bf16[64,4096]{1,0:T(8,128)(2,1)S(1)}, bf16[64,4096]{1,0:T(8,128)(2,1)S(1)}, u32[]{:S(2)}, u32[]{:S(2)}) collective-permute-start(bf16[64,4096]{1,0:T(8,128)(2,1)S(1)} %fusion.5), channel_id=1, source_target_pairs={{0,32},{32,64},{64,96},{96,128},{128,160},{160,192},{192,224},{1,3... | collective-permute-start | bytes 1572872 | tf_op jit(solution)/shard_map/ppermute | solution.py:62
  161.8 11.2 %collective-permute-done.2 = bf16[64,4096]{1,0:T(8,128)(2,1)S(1)} collective-permute-done((bf16[64,4096]{1,0:T(8,128)(2,1)S(1)}, bf16[64,4096]{1,0:T(8,128)(2,1)S(1)}, u32[]{:S(2)}, u32[]{:S(2)}) %collective-permute-start.2) | collective-permute-done | bytes 524320 | tf_op jit(solution)/shard_map/ppermute | solution.py:62
  173.8 1.4 collective-permute-start.3
  175.1 4.4 %collective-permute-done.3 = bf16[20,4096]{1,0:T(8,128)(2,1)S(1)} collective-permute-done((bf16[20,4096]{1,0:T(8,128)(2,1)S(1)}, bf16[20,4096]{1,0:T(8,128)(2,1)S(1)}, u32[]{:S(2)}, u32[]{:S(2)}) %collective-permute-start.3) | collective-permute-done | bytes 163872 | tf_op jit(solution)/shard_map/ppermute | solution.py:47
  180.4 42.9 %all-gather.5.cloned.1.call-done = bf16[640,4096]{1,0:T(8,128)(2,1)} async-done(((bf16[40,4096]{1,0:T(8,128)(2,1)}), bf16[640,4096]{1,0:T(8,128)(2,1)}) %all-gather.5.cloned.1.call-update) | async-done | bytes 5242896 | tf_op jit(solution)/shard_map/all_gather | solution.py:49
  223.3 6.6 %fusion.9 = f32[640,448]{0,1:T(8,128)S(1)} fusion(bf16[640,4096]{1,0:T(8,128)(2,1)} %all-gather.5.cloned.1.call-done, bf16[1,4096,448]{1,2,0:T(8,128)(2,1)} %param.12), kind=kOutput, calls=%fused_computation.15 | convolution fusion | flops 2348810240 | bytes 10059776 | tf_op jit(solution)/shard_map/dot_general | solution.py:51
  229.9 14.8 %convolution_convert_fusion = bf16[640,4096]{1,0:T(8,128)(2,1)} fusion(bf16[1,448,4096]{2,1,0:T(8,128)(2,1)} %param.13, f32[640,448]{0,1:T(8,128)S(1)} %fusion.9, bf16[640,4096]{1,0:T(8,128)(2,1)} %all-gather.5.cloned.1.call-done, bf16[1,4096,448]{1,2,0:T(8,128)(2,1)} %param.11), kind=kOutput, calls=%fused_computation | convolution fusion | flops 4701962240 | bytes 18972672 | tf_op jit(solution)/shard_map/dot_general | solution.py:53
  244.7 64.0 %reduce-scatter.5.cloned.1.call-done = bf16[40,4096]{1,0:T(8,128)(2,1)} async-done(((bf16[640,4096]{1,0:T(8,128)(2,1)}), bf16[40,4096]{1,0:T(8,128)(2,1)}) %reduce-scatter.5.cloned.1.call-update) | async-done | bytes 327696 | tf_op jit(solution)/shard_map/reduce_scatter | solution.py:54
  308.7 1.1 fusion.76
  309.8 1.1 collective-permute-start.4
  310.9 4.7 %collective-permute-done.4 = bf16[20,4096]{1,0:T(8,128)(2,1)S(1)} collective-permute-done((bf16[20,4096]{1,0:T(8,128)(2,1)S(1)}, bf16[20,4096]{1,0:T(8,128)(2,1)S(1)}, u32[]{:S(2)}, u32[]{:S(2)}) %collective-permute-start.4) | collective-permute-done | bytes 163872 | tf_op jit(solution)/shard_map/ppermute | solution.py:55
  316.2 1.1 maximum_bitcast_fusion
  (46 shorter events, 6.0 us)
Async XLA Ops:
  6.5 58.6 %all-gather.3.cloned.1.call-start = ((), (), s32[]{:S(2)}) async-start(), calls=%async_computation.2 | async-start | bytes 5570560 | tf_op jit(solution)/shard_map/all_gather | solution.py:49
  11.5 6.7 %collective-permute-start = (bf16[20,4096]{1,0:T(8,128)(2,1)S(1)}, bf16[20,4096]{1,0:T(8,128)(2,1)S(1)}, u32[]{:S(2)}, u32[]{:S(2)}) collective-permute-start(bf16[20,4096]{1,0:T(8,128)(2,1)S(1)} %get-tuple-element.23), channel_id=1, source_target_pairs={{0,16},{16,0},{1,17},{17,1},{2,18},{18,2},{3,19},{19,3},{4,20},{20... | collective-permute-start | bytes 491528 | tf_op jit(solution)/shard_map/ppermute | solution.py:47
  19.0 131.5 %reduce-scatter.3.cloned.1.call-start = ((), (), s32[]{:S(2)}) async-start(), calls=%async_computation.3 | async-start | bytes 5570560 | tf_op jit(solution)/shard_map/reduce_scatter | solution.py:54
  86.5 0.7 copy-start.2
  86.5 71.0 %copy-start = (bf16[1,64,4096]{2,1,0:T(8,128)(2,1)S(1)}, bf16[1,64,4096]{2,1,0:T(8,128)(2,1)}, u32[]{:S(2)}) copy-start(bf16[1,64,4096]{2,1,0:T(8,128)(2,1)} %param.8) | copy-start | bytes 1572868
  86.5 86.5 %copy-start.1 = (bf16[1,64,4096]{2,1,0:T(8,128)(2,1)S(1)}, bf16[1,64,4096]{2,1,0:T(8,128)(2,1)}, u32[]{:S(2)}) copy-start(bf16[1,64,4096]{2,1,0:T(8,128)(2,1)} %param.9) | copy-start | bytes 1572868
  86.5 86.8 %copy-start.3 = (f32[1,4096]{1,0:T(1,128)S(1)}, f32[1,4096]{1,0:T(1,128)}, u32[]{:S(2)}) copy-start(f32[1,4096]{1,0:T(1,128)} %param.10) | copy-start | bytes 49156
  86.6 136.7 %all-gather.5.cloned.1.call-start = ((), (), s32[]{:S(2)}) async-start(), calls=%async_computation.4 | async-start | bytes 5570560 | tf_op jit(solution)/shard_map/all_gather | solution.py:49
  151.6 5.9 %collective-permute-start.1 = (bf16[20,4096]{1,0:T(8,128)(2,1)S(1)}, bf16[20,4096]{1,0:T(8,128)(2,1)S(1)}, u32[]{:S(2)}, u32[]{:S(2)}) collective-permute-start(bf16[20,4096]{1,0:T(8,128)(2,1)S(1)} %get-tuple-element.21), channel_id=1, source_target_pairs={{0,16},{16,0},{1,17},{17,1},{2,18},{18,2},{3,19},{19,3},{4,20},{20... | collective-permute-start | bytes 491528 | tf_op jit(solution)/shard_map/ppermute | solution.py:55
  158.2 14.8 %collective-permute-start.2 = (bf16[64,4096]{1,0:T(8,128)(2,1)S(1)}, bf16[64,4096]{1,0:T(8,128)(2,1)S(1)}, u32[]{:S(2)}, u32[]{:S(2)}) collective-permute-start(bf16[64,4096]{1,0:T(8,128)(2,1)S(1)} %fusion.5), channel_id=1, source_target_pairs={{0,32},{32,64},{64,96},{96,128},{128,160},{160,192},{192,224},{1,3... | collective-permute-start | bytes 1572872 | tf_op jit(solution)/shard_map/ppermute | solution.py:62
  173.8 5.8 %collective-permute-start.3 = (bf16[20,4096]{1,0:T(8,128)(2,1)S(1)}, bf16[20,4096]{1,0:T(8,128)(2,1)S(1)}, u32[]{:S(2)}, u32[]{:S(2)}) collective-permute-start(bf16[20,4096]{1,0:T(8,128)(2,1)S(1)} %get-tuple-element.19), channel_id=1, source_target_pairs={{0,16},{16,0},{1,17},{17,1},{2,18},{18,2},{3,19},{19,3},{4,20},{20... | collective-permute-start | bytes 491528 | tf_op jit(solution)/shard_map/ppermute | solution.py:47
  180.3 128.4 %reduce-scatter.5.cloned.1.call-start = ((), (), s32[]{:S(2)}) async-start(), calls=%async_computation.5 | async-start | bytes 5570560 | tf_op jit(solution)/shard_map/reduce_scatter | solution.py:54
  309.8 5.8 %collective-permute-start.4 = (bf16[20,4096]{1,0:T(8,128)(2,1)S(1)}, bf16[20,4096]{1,0:T(8,128)(2,1)S(1)}, u32[]{:S(2)}, u32[]{:S(2)}) collective-permute-start(bf16[20,4096]{1,0:T(8,128)(2,1)S(1)} %get-tuple-element.17), channel_id=1, source_target_pairs={{0,16},{16,0},{1,17},{17,1},{2,18},{18,2},{3,19},{19,3},{4,20},{20... | collective-permute-start | bytes 491528 | tf_op jit(solution)/shard_map/ppermute | solution.py:55
Sparse Core Ops, SparseCore 0:
  19.1 45.9 all-gather.2
  86.7 63.7 reduce-scatter.2
  180.4 42.8 all-gather.4
  244.8 63.8 reduce-scatter.4

commit v2 on v1

--- a/solution.py
+++ b/solution.py
@@ -1,6 +1,8 @@
 import jax
 import jax.numpy as jnp
 from jax import lax
+from jax.experimental import pallas as pl
+from jax.experimental.pallas import tpu as pltpu
 from jax.sharding import Mesh, PartitionSpec as P
 
 EXP_WIN = 2
@@ -24,13 +26,118 @@
     return dispatch_table, combine_table
 
 
+def shift(x, axis, by):
+    n = lax.axis_size(axis)
+    return lax.ppermute(x, axis, [(i, (i + by) % n) for i in range(n)])
+
+
+CUT = 24
+SPLIT = 2
+
+
+def ffn_kernel(rows, ga, ua, da, gb, ub, db, out, gbuf, ubuf, dbuf, hid, hid_t, gsem, usem, dsem):
+    blk = gbuf.shape[1]
+    units = da.shape[0]
+    f32 = jnp.float32
+    for i, (g, u) in enumerate(((ga, ua), (gb, ub))):
+        for k in range(SPLIT):
+            at = i * SPLIT + k
+            pltpu.make_async_copy(g.at[pl.ds(k * blk, blk)], gbuf.at[at], gsem.at[at]).start()
+            pltpu.make_async_copy(u.at[pl.ds(k * blk, blk)], ubuf.at[at], usem.at[at]).start()
+    downs = [pltpu.make_async_copy(d, dbuf.at[pl.ds(i * units, units)], dsem.at[i]) for i, d in enumerate((da, db))]
+    for d in downs:
+        d.start()
+    dims = (((1,), (1,)), ((), ()))
+
+    def hidden_block(j, carry):
+        pltpu.make_async_copy(ga.at[pl.ds(0, blk)], gbuf.at[j], gsem.at[j]).wait()
+        gv = lax.dot_general(gbuf[j], rows[...], dims, preferred_element_type=f32)
+        pltpu.make_async_copy(ua.at[pl.ds(0, blk)], ubuf.at[j], usem.at[j]).wait()
+        uv = lax.dot_general(ubuf[j], rows[...], dims, preferred_element_type=f32)
+        hid[j] = (gv / (1.0 + jnp.exp(-gv)) * uv).astype(jnp.bfloat16)
+        return carry
+
+    lax.fori_loop(0, 2 * SPLIT, hidden_block, 0)
+    hid_t[...] = hid[...].reshape(2 * units, rows.shape[0]).T
+    for d in downs:
+        d.wait()
+    cols = 1024
+
+    def out_block(n, carry):
+        at = pl.multiple_of(n * cols, cols)
+        v = jnp.dot(hid_t[...], dbuf[:, pl.ds(at, cols)], preferred_element_type=f32)
+        out[:, pl.ds(at, cols)] = v.astype(jnp.bfloat16)
+        return carry
+
+    lax.fori_loop(0, out.shape[1] // cols, out_block, 0)
+
+
+def ffn(parts, weights):
+    rows = jnp.concatenate(parts, axis=0)
+    r, d = rows.shape
+    (ga, ua, da), (gb, ub, db) = weights
+    units = da.shape[0]
+    blk = units // SPLIT
+    bf16 = jnp.bfloat16
+    hbm = pl.BlockSpec(memory_space=pltpu.HBM)
+    return pl.pallas_call(
+        ffn_kernel,
+        out_shape=jax.ShapeDtypeStruct((r, d), bf16),
+        in_specs=[pl.BlockSpec(memory_space=pltpu.VMEM)] + [hbm] * 6,
+        out_specs=pl.BlockSpec(memory_space=pltpu.VMEM),
+        scratch_shapes=[
+            pltpu.VMEM((2 * SPLIT, blk, d), bf16),
+            pltpu.VMEM((2 * SPLIT, blk, d), bf16),
+            pltpu.VMEM((2 * units, d), bf16),
+            pltpu.VMEM((2 * SPLIT, blk, r), bf16),
+            pltpu.VMEM((r, 2 * units), bf16),
+            pltpu.SemaphoreType.DMA((2 * SPLIT,)),
+            pltpu.SemaphoreType.DMA((2 * SPLIT,)),
+            pltpu.SemaphoreType.DMA((2,)),
+        ],
+        cost_estimate=pl.CostEstimate(flops=12 * r * d * units, transcendentals=2 * r * units,
+                                      bytes_accessed=12 * units * d + 4 * r * d),
+        compiler_params=pltpu.CompilerParams(vmem_limit_bytes=44 * 1024 * 1024),
+        name="ffn",
+    )(rows, ga, ua, da, gb, ub, db)
+
+
+def mixed_experts(block, weights):
+    f32, bf16 = jnp.float32, jnp.bfloat16
+    half = lax.axis_size("z") // 2
+    n = block.shape[0]
+    up, dn = [block], [block]
+    for s in range(1, half):
+        up.append(shift(up[-1], "z", 1))
+        dn.append(shift(dn[-1], "z", -1))
+    near = [block]
+    for s in range(1, half - 1):
+        near += [up[s], dn[s]]
+    near_part = ffn(near, weights)
+    up[-1], dn[-1], near_part = lax.optimization_barrier((up[-1], dn[-1], near_part))
+    far = [shift(up[-1][:CUT], "z", 1), shift(dn[-1][CUT:], "z", -1)]
+    far_part = ffn([up[-1], dn[-1]] + far, weights)
+    a = shift(far_part[2 * n:2 * n + CUT], "z", 1)
+    b = shift(far_part[2 * n + CUT:], "z", -1)
+    pd, pu = far_part[:n], far_part[n:2 * n]
+    a = jnp.concatenate([(pu[:CUT].astype(f32) + a).astype(bf16), pu[CUT:]], axis=0)
+    b = jnp.concatenate([pd[:CUT], (pd[CUT:].astype(f32) + b).astype(bf16)], axis=0)
+    for s in range(half - 2, -1, -1):
+        a, b = shift(a, "z", 1), shift(b, "z", -1)
+        if s:
+            at = n * (2 * s - 1)
+            pd, pu = near_part[at:at + n], near_part[at + n:at + 2 * n]
+            a = (pu.astype(f32) + a).astype(bf16)
+            b = (pd.astype(f32) + b).astype(bf16)
+    return near_part[:n].astype(f32) + a + b
+
+
 def shards(initial, arriving, gains, gate_w, up_w, down_w, pairs, shares):
     section_pos = lax.axis_index("section")
     y_pos = lax.axis_index("y")
     gain = gains[0]
-    gate_cols = gate_w[0]
-    up_cols = up_w[0]
-    down_rows = down_w[0]
+    mine = (gate_w[0].T, up_w[0].T, down_w[0])
+    weights = (mine, tuple(shift(w, "core", 1) for w in mine))
     current = initial[0]
     experts = jnp.stack([y_pos, 1 - y_pos]).astype(jnp.int32)
     swap = [(0, 1), (1, 0)]
@@ -46,12 +153,7 @@
         own, other = send_rows[:CAP], send_rows[CAP:]
         got = lax.ppermute(other, "y", swap)
         block = jnp.concatenate([own, got], axis=0)
-        rows = lax.all_gather(block, ("z", "core"), axis=0, tiled=True)
-        gate_pre = jnp.dot(rows, gate_cols, preferred_element_type=jnp.float32)
-        up_pre = jnp.dot(rows, up_cols, preferred_element_type=jnp.float32)
-        hidden = (jax.nn.silu(gate_pre) * up_pre).astype(jnp.bfloat16)
-        partial = jnp.dot(hidden, down_rows, preferred_element_type=jnp.float32).astype(jnp.bfloat16)
-        summed = lax.psum_scatter(partial, ("z", "core"), scatter_dimension=0, tiled=True)
+        summed = mixed_experts(block, weights).astype(jnp.bfloat16)
         back = lax.ppermute(summed[CAP:], "y", swap)
         both = jnp.concatenate([summed[:CAP], back], axis=0)
         mixture = jnp.dot(comb, both.astype(jnp.float32), precision=lax.Precision.HIGHEST)

time: 324 us -> 279 us (0.86); the launches traced: 324 us -> 274 us
  waiting for transfers between devices: 246 us -> 133 us
  starting transfers between devices: 8.82 us -> 67.6 us
  Pallas kernels: 0 us -> 47.2 us
  matrix products: 45.8 us -> 3 us
  local copies, waits for them, and re-layouts: 4.41 us -> 17.7 us
  between operations: 13.3 us -> 0.84 us
    reduce_scatter x2 -> x0, waiting for transfers between devices: 127 us -> none  [shards(): lax.psum_scatter(partial, ('z', 'core'), scatter_dimension=0, tiled=True)]
    ppermute x0 -> x35, waiting for transfers between devices: none -> 102 us  [shift(): return lax.ppermute(x, axis, [(i, (i + by) % n) for i in range(n)])]
    all_gather x2 -> x0, waiting for transfers between devices: 89 us -> none  [shards(): rows = lax.all_gather(block, ('z', 'core'), axis=0, tiled=True)]
    ppermute x0 -> x35, starting transfers between devices: none -> 58.7 us  [shift(): return lax.ppermute(x, axis, [(i, (i + by) % n) for i in range(n)])]
    pallas_call x0 -> x4, Pallas kernels: none -> 47.2 us  [ffn(): pl.pallas_call(ffn_kernel, out_shape=jax.ShapeDtypeStruct((r, d), bf16),...]
    dot_general x4 -> x0, matrix products: 42.8 us -> none  [the longest x2 29.5 us: shards(): jnp.dot(hidden, down_rows, preferred_element_type=jnp.float32)]
    concatenate x0 -> x2, local copies, waits for them, and re-layouts: none -> 11.7 us  [ffn(): rows = jnp.concatenate(parts, axis=0)]
    unnamed x8 -> x24, local copies, waits for them, and re-layouts: 0.6 us -> 4.12 us
  transfers between devices with their start and end apart: 9 -> 40, of which waited for: 9 -> 26; matrix products, arithmetic and copies ran while one was open for 0% -> 6% of each run, Pallas kernels for 0% -> 9%
where the time goes in v2:
time: 279 us; the launch traced here: 274 us
  waiting for transfers between devices  133 us (48%)
  starting transfers between devices  67.6 us (24%)
  Pallas kernels  47.2 us (17%)
  local copies, waits for them, and re-layouts  17.7 us (6%)
  other arithmetic  4.87 us (2%)
  matrix products  3 us (1%)
    ppermute x35, waiting for transfers between devices, shift(): return lax.ppermute(x, axis, [(i, (i + by) % n) for i in range(n)])  102 us
    ppermute x35, starting transfers between devices, shift(): return lax.ppermute(x, axis, [(i, (i + by) % n) for i in range(n)])  58.7 us
    pallas_call x4, Pallas kernels, ffn(): pl.pallas_call(ffn_kernel, out_shape=jax.ShapeDtypeStruct((r, d), bf16),...  47.2 us
    concatenate x2, local copies, waits for them, and re-layouts, ffn(): rows = jnp.concatenate(parts, axis=0)  11.7 us
    ppermute x1, waiting for transfers between devices, shards(): passed = lax.ppermute(layer_out, 'section', fwd)  11 us
    ppermute x2, waiting for transfers between devices, shards(): got = lax.ppermute(other, 'y', swap)  10.4 us
    ppermute x2, waiting for transfers between devices, shards(): back = lax.ppermute(summed[CAP:], 'y', swap)  8.76 us
  transfers between devices with their start and end apart: 40, of which 26 were waited for; matrix products, arithmetic and copies ran while one was open for 6% of the time, Pallas kernels for 9%

profile of v2, /device:TPU:16, one launch (start us, length us, event | category | flops | bytes accessed | tf_op | source)
XLA Modules:
  0.0 273.9 jit_solution(7566215806022699049)
XLA Ops:
  6.8 6.0 %collective-permute-done = bf16[20,4096]{1,0:T(8,128)(2,1)S(1)} collective-permute-done((bf16[20,4096]{1,0:T(8,128)(2,1)S(1)}, bf16[20,4096]{1,0:T(8,128)(2,1)S(1)}, u32[]{:S(2)}, u32[]{:S(2)}) %collective-permute-start) | collective-permute-done | bytes 163872 | tf_op jit(solution)/shard_map/ppermute | solution.py:154
  18.9 7.4 %collective-permute-done.1 = bf16[40,4096]{1,0:T(8,128)(2,1)S(1)} collective-permute-done((bf16[40,4096]{1,0:T(8,128)(2,1)S(1)}, bf16[40,4096]{1,0:T(8,128)(2,1)S(1)}, u32[]{:S(2)}, u32[]{:S(2)}) %collective-permute-start.1) | collective-permute-done | bytes 327712 | tf_op jit(solution)/shard_map/ppermute | solution.py:31
  29.6 6.7 %collective-permute-done.2 = bf16[40,4096]{1,0:T(8,128)(2,1)S(1)} collective-permute-done((bf16[40,4096]{1,0:T(8,128)(2,1)S(1)}, bf16[40,4096]{1,0:T(8,128)(2,1)S(1)}, u32[]{:S(2)}, u32[]{:S(2)}) %collective-permute-start.2) | collective-permute-done | bytes 327712 | tf_op jit(solution)/shard_map/ppermute | solution.py:31
  45.2 12.3 %ffn.4 = bf16[200,4096]{1,0:T(8,128)(2,1)S(1)} custom-call(bf16[200,4096]{1,0:T(8,128)(2,1)S(1)} %concatenate.39.rows, bf16[448,4096]{1,0:T(8,128)(2,1)S(1)} %bitcast.69, bf16[448,4096]{1,0:T(8,128)(2,1)} %bitcast.74, bf16[448,4096]{1,0:T(8,128)(2,1)} %bitcast.79, bf16[448,4096]{1,0:T(8,128)(2,1)} %collective-permute-done.7.gb, ...), custom_call_target="tpu_custom_call" | custom-call | flops 4404019200 | bytes 25296896 | tf_op jit(solution)/shard_map/ffn/pallas_call | solution.py:83
  64.7 11.3 %ffn.5 = bf16[120,4096]{1,0:T(8,128)(2,1)S(1)} custom-call(bf16[120,4096]{1,0:T(8,128)(2,1)S(1)} %pad_maximum_fusion.rows, bf16[448,4096]{1,0:T(8,128)(2,1)S(1)} %bitcast.70, bf16[448,4096]{1,0:T(8,128)(2,1)S(1)} %bitcast.76, bf16[448,4096]{1,0:T(8,128)(2,1)} %bitcast.80, bf16[448,4096]{1,0:T(8,128)(2,1)} %collective-permute-done.7.gb, ...), custom_call_target="tpu_custom_call" | custom-call | flops 2642411520 | bytes 23986176 | tf_op jit(solution)/shard_map/ffn/pallas_call | solution.py:83
  81.5 5.6 %collective-permute-done.12 = bf16[24,4096]{1,0:T(8,128)(2,1)S(1)} collective-permute-done((bf16[24,4096]{1,0:T(8,128)(2,1)S(1)}, bf16[24,4096]{1,0:T(8,128)(2,1)S(1)}, u32[]{:S(2)}, u32[]{:S(2)}) %collective-permute-start.12) | collective-permute-done | bytes 196640 | tf_op jit(solution)/shard_map/ppermute | solution.py:31
  90.7 7.3 %collective-permute-done.13 = bf16[40,4096]{1,0:T(8,128)(2,1)S(1)} collective-permute-done((bf16[40,4096]{1,0:T(8,128)(2,1)S(1)}, bf16[40,4096]{1,0:T(8,128)(2,1)S(1)}, u32[]{:S(2)}, u32[]{:S(2)}) %collective-permute-start.13) | collective-permute-done | bytes 327712 | tf_op jit(solution)/shard_map/ppermute | solution.py:31
  98.1 11.6 %collective-permute-done.14 = bf16[40,4096]{1,0:T(8,128)(2,1)S(1)} collective-permute-done((bf16[40,4096]{1,0:T(8,128)(2,1)S(1)}, bf16[40,4096]{1,0:T(8,128)(2,1)S(1)}, u32[]{:S(2)}, u32[]{:S(2)}) %collective-permute-start.14) | collective-permute-done | bytes 327712 | tf_op jit(solution)/shard_map/ppermute | solution.py:31
  112.0 5.0 %collective-permute-done.18 = bf16[40,4096]{1,0:T(8,128)(2,1)S(1)} collective-permute-done((bf16[40,4096]{1,0:T(8,128)(2,1)S(1)}, bf16[40,4096]{1,0:T(8,128)(2,1)S(1)}, u32[]{:S(2)}, u32[]{:S(2)}) %collective-permute-start.18) | collective-permute-done | bytes 327712 | tf_op jit(solution)/shard_map/ppermute | solution.py:31
  118.5 5.8 %collective-permute-done.19 = bf16[40,4096]{1,0:T(8,128)(2,1)S(1)} collective-permute-done((bf16[40,4096]{1,0:T(8,128)(2,1)S(1)}, bf16[40,4096]{1,0:T(8,128)(2,1)S(1)}, u32[]{:S(2)}, u32[]{:S(2)}) %collective-permute-start.19) | collective-permute-done | bytes 327712 | tf_op jit(solution)/shard_map/ppermute | solution.py:31
  125.9 4.4 %collective-permute-done.20 = bf16[20,4096]{1,0:T(8,128)(2,1)S(1)} collective-permute-done((bf16[20,4096]{1,0:T(8,128)(2,1)S(1)}, bf16[20,4096]{1,0:T(8,128)(2,1)S(1)}, u32[]{:S(2)}, u32[]{:S(2)}) %collective-permute-start.20) | collective-permute-done | bytes 163872 | tf_op jit(solution)/shard_map/ppermute | solution.py:157
  134.6 11.0 %collective-permute-done.21 = bf16[64,4096]{1,0:T(8,128)(2,1)S(1)} collective-permute-done((bf16[64,4096]{1,0:T(8,128)(2,1)S(1)}, bf16[64,4096]{1,0:T(8,128)(2,1)S(1)}, u32[]{:S(2)}, u32[]{:S(2)}) %collective-permute-start.21) | collective-permute-done | bytes 524320 | tf_op jit(solution)/shard_map/ppermute | solution.py:164
  147.7 4.4 %collective-permute-done.22 = bf16[20,4096]{1,0:T(8,128)(2,1)S(1)} collective-permute-done((bf16[20,4096]{1,0:T(8,128)(2,1)S(1)}, bf16[20,4096]{1,0:T(8,128)(2,1)S(1)}, u32[]{:S(2)}, u32[]{:S(2)}) %collective-permute-start.22) | collective-permute-done | bytes 163872 | tf_op jit(solution)/shard_map/ppermute | solution.py:154
  152.2 11.8 %collective-permute-start.26 = (bf16[40,4096]{1,0:T(8,128)(2,1)S(1)}, bf16[40,4096]{1,0:T(8,128)(2,1)S(1)}, u32[]{:S(2)}, u32[]{:S(2)}) collective-permute-start(bf16[40,4096]{1,0:T(8,128)(2,1)S(1)} %pad_maximum_fusion.5), channel_id=1, source_target_pairs={{0,14},{2,0},{4,2},{6,4},{8,6},{10,8},{12,10},{14,12},{1,15},{3,1}... | collective-permute-start | bytes 983048 | tf_op jit(solution)/shard_map/ppermute | solution.py:31
  164.1 4.6 %collective-permute-done.26 = bf16[40,4096]{1,0:T(8,128)(2,1)S(1)} collective-permute-done((bf16[40,4096]{1,0:T(8,128)(2,1)S(1)}, bf16[40,4096]{1,0:T(8,128)(2,1)S(1)}, u32[]{:S(2)}, u32[]{:S(2)}) %collective-permute-start.26) | collective-permute-done | bytes 327712 | tf_op jit(solution)/shard_map/ppermute | solution.py:31
  172.5 5.4 %collective-permute-done.27 = bf16[40,4096]{1,0:T(8,128)(2,1)} collective-permute-done((bf16[40,4096]{1,0:T(8,128)(2,1)S(1)}, bf16[40,4096]{1,0:T(8,128)(2,1)}, u32[]{:S(2)}, u32[]{:S(2)}) %collective-permute-start.27) | collective-permute-done | bytes 327712 | tf_op jit(solution)/shard_map/ppermute | solution.py:31
  177.8 8.1 %concatenate.45.rows = bf16[200,4096]{1,0:T(8,128)(2,1)S(1)} concatenate(bf16[20,4096]{1,0:T(8,128)(2,1)S(1)} %get-tuple-element.42, bf16[20,4096]{1,0:T(8,128)(2,1)S(1)} %collective-permute-done.22, bf16[40,4096]{1,0:T(8,128)(2,1)} %copy-done.7, bf16[40,4096]{1,0:T(8,128)(2,1)} %copy-done.9, bf16[40,4096]{1,0:T(8,128)(2,1)} %collective-permute-done.24, ...), dimensions={0} | concatenate | bytes 3276800 | tf_op jit(solution)/shard_map/concatenate | solution.py:76
  191.8 12.3 %ffn.6 = bf16[200,4096]{1,0:T(8,128)(2,1)S(1)} custom-call(bf16[200,4096]{1,0:T(8,128)(2,1)S(1)} %concatenate.45.rows, bf16[448,4096]{1,0:T(8,128)(2,1)S(1)} %bitcast.71, bf16[448,4096]{1,0:T(8,128)(2,1)} %bitcast.75, bf16[448,4096]{1,0:T(8,128)(2,1)} %bitcast.81, bf16[448,4096]{1,0:T(8,128)(2,1)} %collective-permute-done.7.gb, ...), custom_call_target="tpu_custom_call" | custom-call | flops 4404019200 | bytes 25296896 | tf_op jit(solution)/shard_map/ffn/pallas_call | solution.py:83
  212.2 11.3 %ffn.7 = bf16[120,4096]{1,0:T(8,128)(2,1)S(1)} custom-call(bf16[120,4096]{1,0:T(8,128)(2,1)S(1)} %pad_maximum_fusion.1.rows, bf16[448,4096]{1,0:T(8,128)(2,1)S(1)} %bitcast.72, bf16[448,4096]{1,0:T(8,128)(2,1)S(1)} %bitcast.77, bf16[448,4096]{1,0:T(8,128)(2,1)} %bitcast.82, bf16[448,4096]{1,0:T(8,128)(2,1)} %collective-permute-done.7.gb, ...), custom_call_target="tpu_custom_call" | custom-call | flops 2642411520 | bytes 23986176 | tf_op jit(solution)/shard_map/ffn/pallas_call | solution.py:83
  229.1 5.3 %collective-permute-done.31 = bf16[24,4096]{1,0:T(8,128)(2,1)S(1)} collective-permute-done((bf16[24,4096]{1,0:T(8,128)(2,1)S(1)}, bf16[24,4096]{1,0:T(8,128)(2,1)S(1)}, u32[]{:S(2)}, u32[]{:S(2)}) %collective-permute-start.31) | collective-permute-done | bytes 196640 | tf_op jit(solution)/shard_map/ppermute | solution.py:31
  237.9 4.9 %collective-permute-done.32 = bf16[40,4096]{1,0:T(8,128)(2,1)S(1)} collective-permute-done((bf16[40,4096]{1,0:T(8,128)(2,1)S(1)}, bf16[40,4096]{1,0:T(8,128)(2,1)S(1)}, u32[]{:S(2)}, u32[]{:S(2)}) %collective-permute-start.32) | collective-permute-done | bytes 327712 | tf_op jit(solution)/shard_map/ppermute | solution.py:31
  243.2 8.3 %collective-permute-done.33 = bf16[40,4096]{1,0:T(8,128)(2,1)S(1)} collective-permute-done((bf16[40,4096]{1,0:T(8,128)(2,1)S(1)}, bf16[40,4096]{1,0:T(8,128)(2,1)S(1)}, u32[]{:S(2)}, u32[]{:S(2)}) %collective-permute-start.33) | collective-permute-done | bytes 327712 | tf_op jit(solution)/shard_map/ppermute | solution.py:31
  253.8 5.0 %collective-permute-done.37 = bf16[40,4096]{1,0:T(8,128)(2,1)S(1)} collective-permute-done((bf16[40,4096]{1,0:T(8,128)(2,1)S(1)}, bf16[40,4096]{1,0:T(8,128)(2,1)S(1)}, u32[]{:S(2)}, u32[]{:S(2)}) %collective-permute-start.37) | collective-permute-done | bytes 327712 | tf_op jit(solution)/shard_map/ppermute | solution.py:31
  260.2 5.9 %collective-permute-done.38 = bf16[40,4096]{1,0:T(8,128)(2,1)S(1)} collective-permute-done((bf16[40,4096]{1,0:T(8,128)(2,1)S(1)}, bf16[40,4096]{1,0:T(8,128)(2,1)S(1)}, u32[]{:S(2)}, u32[]{:S(2)}) %collective-permute-start.38) | collective-permute-done | bytes 327712 | tf_op jit(solution)/shard_map/ppermute | solution.py:31
  (148 shorter events, 91.3 us)
Async XLA Ops:
  0.0 43.2 %collective-permute-start.7 = (bf16[448,4096]{1,0:T(8,128)(2,1)}, bf16[448,4096]{1,0:T(8,128)(2,1)}, u32[]{:S(2)}, u32[]{:S(2)}) collective-permute-start(bf16[448,4096]{1,0:T(8,128)(2,1)} %bitcast.68), channel_id=1, source_target_pairs={{0,1},{1,0},{2,3},{3,2},{4,5},{5,4},{6,7},{7,6},{8,9},{9,8},{10,11... | collective-permute-start | bytes 11010056 | tf_op jit(solution)/shard_map/ppermute | solution.py:31
  0.0 43.2 %collective-permute-start.8 = (bf16[448,4096]{1,0:T(8,128)(2,1)}, bf16[448,4096]{1,0:T(8,128)(2,1)}, u32[]{:S(2)}, u32[]{:S(2)}) collective-permute-start(bf16[448,4096]{1,0:T(8,128)(2,1)} %bitcast.73), channel_id=1, source_target_pairs={{0,1},{1,0},{2,3},{3,2},{4,5},{5,4},{6,7},{7,6},{8,9},{9,8},{10,11... | collective-permute-start | bytes 11010056 | tf_op jit(solution)/shard_map/ppermute | solution.py:31
  0.5 42.7 %collective-permute-start.9 = (bf16[448,4096]{1,0:T(8,128)(2,1)}, bf16[448,4096]{1,0:T(8,128)(2,1)}, u32[]{:S(2)}, u32[]{:S(2)}) collective-permute-start(bf16[448,4096]{1,0:T(8,128)(2,1)} %bitcast.78), channel_id=1, source_target_pairs={{0,1},{1,0},{2,3},{3,2},{4,5},{5,4},{6,7},{7,6},{8,9},{9,8},{10,11... | collective-permute-start | bytes 11010056 | tf_op jit(solution)/shard_map/ppermute | solution.py:31
  12.9 13.5 %collective-permute-start.1 = (bf16[40,4096]{1,0:T(8,128)(2,1)S(1)}, bf16[40,4096]{1,0:T(8,128)(2,1)S(1)}, u32[]{:S(2)}, u32[]{:S(2)}) collective-permute-start(bf16[40,4096]{1,0:T(8,128)(2,1)S(1)} %pad_maximum_fusion.2), channel_id=1, source_target_pairs={{0,2},{2,4},{4,6},{6,8},{8,10},{10,12},{12,14},{14,0},{1,3},{3,5},... | collective-permute-start | bytes 983048 | tf_op jit(solution)/shard_map/ppermute | solution.py:31
  14.9 11.5 %collective-permute-start.4 = (bf16[40,4096]{1,0:T(8,128)(2,1)S(1)}, bf16[40,4096]{1,0:T(8,128)(2,1)S(1)}, u32[]{:S(2)}, u32[]{:S(2)}) collective-permute-start(bf16[40,4096]{1,0:T(8,128)(2,1)S(1)} %pad_maximum_fusion.2), channel_id=1, source_target_pairs={{0,14},{2,0},{4,2},{6,4},{8,6},{10,8},{12,10},{14,12},{1,15},{3,1}... | collective-permute-start | bytes 983048 | tf_op jit(solution)/shard_map/ppermute | solution.py:31
  26.4 9.9 %collective-permute-start.2 = (bf16[40,4096]{1,0:T(8,128)(2,1)S(1)}, bf16[40,4096]{1,0:T(8,128)(2,1)S(1)}, u32[]{:S(2)}, u32[]{:S(2)}) collective-permute-start(bf16[40,4096]{1,0:T(8,128)(2,1)S(1)} %collective-permute-done.1), channel_id=1, source_target_pairs={{0,2},{2,4},{4,6},{6,8},{8,10},{10,12},{12,14},{14,0},{1,3},{3,5},... | collective-permute-start | bytes 983048 | tf_op jit(solution)/shard_map/ppermute | solution.py:31
  26.4 9.9 %collective-permute-start.5 = (bf16[40,4096]{1,0:T(8,128)(2,1)S(1)}, bf16[40,4096]{1,0:T(8,128)(2,1)S(1)}, u32[]{:S(2)}, u32[]{:S(2)}) collective-permute-start(bf16[40,4096]{1,0:T(8,128)(2,1)S(1)} %collective-permute-done.4), channel_id=1, source_target_pairs={{0,14},{2,0},{4,2},{6,4},{8,6},{10,8},{12,10},{14,12},{1,15},{3,1}... | collective-permute-start | bytes 983048 | tf_op jit(solution)/shard_map/ppermute | solution.py:31
  36.3 21.3 %collective-permute-start.3 = (bf16[40,4096]{1,0:T(8,128)(2,1)S(1)}, bf16[40,4096]{1,0:T(8,128)(2,1)S(1)}, u32[]{:S(2)}, u32[]{:S(2)}) collective-permute-start(bf16[40,4096]{1,0:T(8,128)(2,1)S(1)} %collective-permute-done.2), channel_id=1, source_target_pairs={{0,2},{2,4},{4,6},{6,8},{8,10},{10,12},{12,14},{14,0},{1,3},{3,5},... | collective-permute-start | bytes 983048 | tf_op jit(solution)/shard_map/ppermute | solution.py:31
  39.9 17.7 %collective-permute-start.6 = (bf16[40,4096]{1,0:T(8,128)(2,1)S(1)}, bf16[40,4096]{1,0:T(8,128)(2,1)S(1)}, u32[]{:S(2)}, u32[]{:S(2)}) collective-permute-start(bf16[40,4096]{1,0:T(8,128)(2,1)S(1)} %collective-permute-done.5), channel_id=1, source_target_pairs={{0,14},{2,0},{4,2},{6,4},{8,6},{10,8},{12,10},{14,12},{1,15},{3,1}... | collective-permute-start | bytes 983048 | tf_op jit(solution)/shard_map/ppermute | solution.py:31
  87.2 10.7 %collective-permute-start.13 = (bf16[40,4096]{1,0:T(8,128)(2,1)S(1)}, bf16[40,4096]{1,0:T(8,128)(2,1)S(1)}, u32[]{:S(2)}, u32[]{:S(2)}) collective-permute-start(bf16[40,4096]{1,0:T(8,128)(2,1)S(1)} %pad_maximum_fusion.3), channel_id=1, source_target_pairs={{0,2},{2,4},{4,6},{6,8},{8,10},{10,12},{12,14},{14,0},{1,3},{3,5},... | collective-permute-start | bytes 983048 | tf_op jit(solution)/shard_map/ppermute | solution.py:31
  87.4 10.8 %collective-permute-start.17 = (bf16[40,4096]{1,0:T(8,128)(2,1)S(1)}, bf16[40,4096]{1,0:T(8,128)(2,1)S(1)}, u32[]{:S(2)}, u32[]{:S(2)}) collective-permute-start(bf16[40,4096]{1,0:T(8,128)(2,1)S(1)} %pad_maximum_fusion.4), channel_id=1, source_target_pairs={{0,14},{2,0},{4,2},{6,4},{8,6},{10,8},{12,10},{14,12},{1,15},{3,1}... | collective-permute-start | bytes 983048 | tf_op jit(solution)/shard_map/ppermute | solution.py:31
  98.0 11.7 %collective-permute-start.14 = (bf16[40,4096]{1,0:T(8,128)(2,1)S(1)}, bf16[40,4096]{1,0:T(8,128)(2,1)S(1)}, u32[]{:S(2)}, u32[]{:S(2)}) collective-permute-start(bf16[40,4096]{1,0:T(8,128)(2,1)S(1)} %add_convert_fusion.9), channel_id=1, source_target_pairs={{0,2},{2,4},{4,6},{6,8},{8,10},{10,12},{12,14},{14,0},{1,3},{3,5},... | collective-permute-start | bytes 983048 | tf_op jit(solution)/shard_map/ppermute | solution.py:31
  110.0 8.5 %collective-permute-start.15 = (bf16[40,4096]{1,0:T(8,128)(2,1)S(1)}, bf16[40,4096]{1,0:T(8,128)(2,1)S(1)}, u32[]{:S(2)}, u32[]{:S(2)}) collective-permute-start(bf16[40,4096]{1,0:T(8,128)(2,1)S(1)} %get-tuple-element.30), channel_id=1, source_target_pairs={{0,2},{2,4},{4,6},{6,8},{8,10},{10,12},{12,14},{14,0},{1,3},{3,5},... | collective-permute-start | bytes 983048 | tf_op jit(solution)/shard_map/ppermute | solution.py:31
  130.9 14.7 %collective-permute-start.21 = (bf16[64,4096]{1,0:T(8,128)(2,1)S(1)}, bf16[64,4096]{1,0:T(8,128)(2,1)S(1)}, u32[]{:S(2)}, u32[]{:S(2)}) collective-permute-start(bf16[64,4096]{1,0:T(8,128)(2,1)S(1)} %fusion.5), channel_id=1, source_target_pairs={{0,32},{32,64},{64,96},{96,128},{128,160},{160,192},{192,224},{1,3... | collective-permute-start | bytes 1572872 | tf_op jit(solution)/shard_map/ppermute | solution.py:164
  152.1 11.9 %collective-permute-start.23 = (bf16[40,4096]{1,0:T(8,128)(2,1)S(1)}, bf16[40,4096]{1,0:T(8,128)(2,1)S(1)}, u32[]{:S(2)}, u32[]{:S(2)}) collective-permute-start(bf16[40,4096]{1,0:T(8,128)(2,1)S(1)} %pad_maximum_fusion.5), channel_id=1, source_target_pairs={{0,2},{2,4},{4,6},{6,8},{8,10},{10,12},{12,14},{14,0},{1,3},{3,5},... | collective-permute-start | bytes 983048 | tf_op jit(solution)/shard_map/ppermute | solution.py:31
  152.2 16.4 %collective-permute-start.26 = (bf16[40,4096]{1,0:T(8,128)(2,1)S(1)}, bf16[40,4096]{1,0:T(8,128)(2,1)S(1)}, u32[]{:S(2)}, u32[]{:S(2)}) collective-permute-start(bf16[40,4096]{1,0:T(8,128)(2,1)S(1)} %pad_maximum_fusion.5), channel_id=1, source_target_pairs={{0,14},{2,0},{4,2},{6,4},{8,6},{10,8},{12,10},{14,12},{1,15},{3,1}... | collective-permute-start | bytes 983048 | tf_op jit(solution)/shard_map/ppermute | solution.py:31
  164.1 8.4 %collective-permute-start.24 = (bf16[40,4096]{1,0:T(8,128)(2,1)S(1)}, bf16[40,4096]{1,0:T(8,128)(2,1)}, u32[]{:S(2)}, u32[]{:S(2)}) collective-permute-start(bf16[40,4096]{1,0:T(8,128)(2,1)S(1)} %collective-permute-done.23), channel_id=1, source_target_pairs={{0,2},{2,4},{4,6},{6,8},{8,10},{10,12},{12,14},{14,0},{1,3},{3,5},... | collective-permute-start | bytes 983048 | tf_op jit(solution)/shard_map/ppermute | solution.py:31
  168.6 9.2 %collective-permute-start.27 = (bf16[40,4096]{1,0:T(8,128)(2,1)S(1)}, bf16[40,4096]{1,0:T(8,128)(2,1)}, u32[]{:S(2)}, u32[]{:S(2)}) collective-permute-start(bf16[40,4096]{1,0:T(8,128)(2,1)S(1)} %collective-permute-done.26), channel_id=1, source_target_pairs={{0,14},{2,0},{4,2},{6,4},{8,6},{10,8},{12,10},{14,12},{1,15},{3,1}... | collective-permute-start | bytes 983048 | tf_op jit(solution)/shard_map/ppermute | solution.py:31
  172.4 31.7 %collective-permute-start.25 = (bf16[40,4096]{1,0:T(8,128)(2,1)}, bf16[40,4096]{1,0:T(8,128)(2,1)S(1)}, u32[]{:S(2)}, u32[]{:S(2)}) collective-permute-start(bf16[40,4096]{1,0:T(8,128)(2,1)} %collective-permute-done.24), channel_id=1, source_target_pairs={{0,2},{2,4},{4,6},{6,8},{8,10},{10,12},{12,14},{14,0},{1,3},{3,5},... | collective-permute-start | bytes 983048 | tf_op jit(solution)/shard_map/ppermute | solution.py:31
  185.9 18.3 %collective-permute-start.28 = (bf16[40,4096]{1,0:T(8,128)(2,1)}, bf16[40,4096]{1,0:T(8,128)(2,1)S(1)}, u32[]{:S(2)}, u32[]{:S(2)}) collective-permute-start(bf16[40,4096]{1,0:T(8,128)(2,1)} %collective-permute-done.27), channel_id=1, source_target_pairs={{0,14},{2,0},{4,2},{6,4},{8,6},{10,8},{12,10},{14,12},{1,15},{3,1}... | collective-permute-start | bytes 983048 | tf_op jit(solution)/shard_map/ppermute | solution.py:31
  225.3 9.1 %collective-permute-start.31 = (bf16[24,4096]{1,0:T(8,128)(2,1)S(1)}, bf16[24,4096]{1,0:T(8,128)(2,1)S(1)}, u32[]{:S(2)}, u32[]{:S(2)}) collective-permute-start(bf16[24,4096]{1,0:T(8,128)(2,1)S(1)} %get-tuple-element.32), channel_id=1, source_target_pairs={{0,2},{2,4},{4,6},{6,8},{8,10},{10,12},{12,14},{14,0},{1,3},{3,5},... | collective-permute-start | bytes 589832 | tf_op jit(solution)/shard_map/ppermute | solution.py:31
  234.6 8.6 %collective-permute-start.36 = (bf16[40,4096]{1,0:T(8,128)(2,1)S(1)}, bf16[40,4096]{1,0:T(8,128)(2,1)S(1)}, u32[]{:S(2)}, u32[]{:S(2)}) collective-permute-start(bf16[40,4096]{1,0:T(8,128)(2,1)S(1)} %pad_maximum_fusion.7), channel_id=1, source_target_pairs={{0,14},{2,0},{4,2},{6,4},{8,6},{10,8},{12,10},{14,12},{1,15},{3,1}... | collective-permute-start | bytes 983048 | tf_op jit(solution)/shard_map/ppermute | solution.py:31
  242.9 8.6 %collective-permute-start.33 = (bf16[40,4096]{1,0:T(8,128)(2,1)S(1)}, bf16[40,4096]{1,0:T(8,128)(2,1)S(1)}, u32[]{:S(2)}, u32[]{:S(2)}) collective-permute-start(bf16[40,4096]{1,0:T(8,128)(2,1)S(1)} %add_convert_fusion.4), channel_id=1, source_target_pairs={{0,2},{2,4},{4,6},{6,8},{8,10},{10,12},{12,14},{14,0},{1,3},{3,5},... | collective-permute-start | bytes 983048 | tf_op jit(solution)/shard_map/ppermute | solution.py:31
  251.8 8.4 %collective-permute-start.34 = (bf16[40,4096]{1,0:T(8,128)(2,1)S(1)}, bf16[40,4096]{1,0:T(8,128)(2,1)S(1)}, u32[]{:S(2)}, u32[]{:S(2)}) collective-permute-start(bf16[40,4096]{1,0:T(8,128)(2,1)S(1)} %get-tuple-element.28), channel_id=1, source_target_pairs={{0,2},{2,4},{4,6},{6,8},{8,10},{10,12},{12,14},{14,0},{1,3},{3,5},... | collective-permute-start | bytes 983048 | tf_op jit(solution)/shard_map/ppermute | solution.py:31
  (28 other events, 294.3 us)
